TPU v7x, 256 devices: a whole 4x4x8 slice. The times are simulated.
256 devices in a mesh: section: 8 (over z_hi, core), batch: 8 (over x, z_lo), tile: 4 (over y).
Axes of the slice: x: 4, y: 4, z: 8 (z_hi: 4, z_lo: 2; z = z_hi * 2 + z_lo), core: 2. Of those that a mesh axis runs over, the one named last changes fastest.
Arguments:
- latents: bfloat16 [32, 4, 32, 1280], P('batch', 'tile'), parts along dimension 0, may hold values from -6 to 6
- prompt_tokens: bfloat16 [32, 77, 2048], P('batch'), parts along dimension 0, may hold values from -6 to 6
- fresh_noise: bfloat16 [1, 32, 4, 32, 1280], P(None, 'batch', 'tile'), parts along dimension 1, may hold values from -6 to 6
- timesteps: int32 [2], replicated, may hold values from 600 to 999
- entry_order: int32 [32], P('batch'), parts along dimension 0, may hold values from 0 to 3, each once
- timestep_weight: bfloat16 [8, 320, 1280], P('section'), may hold values from -0.3125 to 0.3125
- conv_kernel: float32 [8, 9, 1280], P('section'), may hold values from -1 to 1
- norm_gain: float32 [8, 1280], P('section'), may hold values from 0.25 to 1.75
- layer_norm_bias: float32 [8, 1280], P('section'), may hold values from -1.5 to 1.5
- qkv_weight: bfloat16 [8, 1280, 3, 1280], P('section', None, None, 'tile'), may hold values from -0.15625 to 0.15625
- prompt_weight: bfloat16 [8, 2048, 2, 1280], P('section', None, None, 'tile'), may hold values from -0.125 to 0.125
- out_weight: bfloat16 [8, 1280, 1280], P('section', 'tile'), may hold values from -0.15625 to 0.15625
Outputs:
- samples: bfloat16 [32, 4, 32, 1280], P('batch', 'tile', None, 'section'), parts along dimension 0
There are 8 independent parts, one for each index of `batch`. A program takes and returns all parts, laid end to end along the dimension named above; an argument that names none is the same for every part. Nothing has to cross between parts.
All inputs are finite; a program needn't handle non-finite values.
Results may differ from a plain program's by a relative error of at most 0.019.
Values may be sent and summed in bfloat16 or wider, within the bound.
A program may use at most 64 MiB of HBM per device.

v0:
```python
import math

import jax
import jax.numpy as jnp
from jax import lax
from jax.sharding import PartitionSpec as P

HEADS = 20


def extended(cells, sides, width):
    for axis, dim in sides:
        count = lax.axis_size(axis)
        ends = count - 1
        head = lax.slice_in_dim(cells, 0, width, axis=dim)
        tail = lax.slice_in_dim(cells, cells.shape[dim] - width, cells.shape[dim], axis=dim)
        cells = jnp.concatenate(
            [
                lax.ppermute(tail, axis, [(i, (i + 1) % count) for i in range(ends)]),
                cells,
                lax.ppermute(head, axis, [((i + 1) % count, i) for i in range(ends)]),
            ],
            axis=dim,
        )
    return cells


def split_up(shard, dim, count):
    lengths = shard.shape
    parts = shard.reshape(*lengths[:dim], count, lengths[dim] // count, *lengths[dim + 1 :])
    return jnp.moveaxis(parts, dim, 0)


def summed_on_arrival(shard, axis, dim):
    parts = split_up(shard, dim, lax.axis_size(axis))
    arrived = lax.all_to_all(parts, axis, split_axis=0, concat_axis=0, tiled=True)
    return arrived.astype(jnp.float32).sum(axis=0)


def from_behind(shard, axis, by):
    count = lax.axis_size(axis)
    return lax.ppermute(shard, axis, [(i, (i + by) % count) for i in range(count)])


def from_root(shard, axis, root):
    return lax.dynamic_index_in_dim(lax.all_gather(shard, axis), root, 0, keepdims=False)


def noise_plan():
    positions = jnp.arange(1000, dtype=jnp.float32)
    low_root = math.sqrt(0.00085)
    high_root = math.sqrt(0.012)
    roots = low_root + (high_root - low_root) * positions / 999.0
    return jnp.exp(jnp.cumsum(jnp.log(1.0 - roots * roots)))


def time_features(timesteps, half_count):
    exponents = jnp.arange(half_count, dtype=jnp.float32) / half_count
    freq_row = jnp.exp(-math.log(10000.0) * exponents)
    angles = timesteps.astype(jnp.float32)[:, None] * freq_row[None, :]
    return jnp.concatenate([jnp.cos(angles), jnp.sin(angles)], axis=1).astype(jnp.bfloat16)


def pick_scalar(alpha_table, position):
    hits = jnp.arange(alpha_table.shape[0], dtype=jnp.int32) == position
    return jnp.sum(jnp.where(hits, alpha_table, jnp.zeros_like(alpha_table)))


def pick_integer(int_table, position):
    hits = jnp.arange(int_table.shape[0], dtype=jnp.int32) == position
    return jnp.sum(jnp.where(hits, int_table, jnp.zeros_like(int_table)))


def mix_positions(rimmed, kernel_body):
    row_total = rimmed.shape[0] - 2
    col_total = rimmed.shape[1]
    framed = jnp.pad(rimmed.astype(jnp.float32), ((0, 0), (1, 1), (0, 0)))
    mixed = rimmed[1:-1].astype(jnp.float32)
    for offset_row in range(3):
        for offset_col in range(3):
            mixed = (
                mixed
                + kernel_body[3 * offset_row + offset_col]
                * framed[offset_row : offset_row + row_total, offset_col : offset_col + col_total]
            )
    return mixed


def layer_norm(values_in, scale_row, shift_row):
    centre = jnp.mean(values_in, axis=-1, keepdims=True)
    spread = jnp.mean(jnp.square(values_in - centre), axis=-1, keepdims=True)
    return (values_in - centre) * lax.rsqrt(spread + 1e-05) * scale_row + shift_row


def attend(queries, keys_all, values_all, head_count):
    query_count = queries.shape[0]
    key_count = keys_all.shape[0]
    head_width = queries.shape[1] // head_count
    query_heads = queries.reshape(query_count, head_count, head_width)
    key_heads = keys_all.reshape(key_count, head_count, head_width)
    value_heads = values_all.reshape(key_count, head_count, head_width)
    scores = jnp.einsum(
        "qhd,khd->hqk", query_heads, key_heads, preferred_element_type=jnp.float32
    ) / math.sqrt(head_width)
    powers = jnp.exp(scores)
    soft_weights = (powers / jnp.sum(powers, axis=-1, keepdims=True)).astype(jnp.bfloat16)
    attended = jnp.einsum(
        "hqk,khd->qhd", soft_weights, value_heads, preferred_element_type=jnp.float32
    )
    return attended.reshape(query_count, head_count * head_width).astype(jnp.bfloat16)


def per_device(
    latents,
    prompt_tokens,
    fresh_noise,
    timesteps,
    entry_order,
    timestep_weight,
    conv_kernel,
    norm_gain,
    layer_norm_bias,
    qkv_weight,
    prompt_weight,
    out_weight,
):
    section_count = lax.axis_size("section")
    tile_count = lax.axis_size("tile")
    section_index = lax.axis_index("section")
    micro_count, rows_here, cols_here, width_all = latents.shape
    token_here = rows_here * cols_here
    chain_total = timesteps.shape[0]
    alpha_table = noise_plan()
    feature_rows = time_features(timesteps, timestep_weight.shape[1] // 2)
    timestep_embedding_all = jnp.dot(
        feature_rows, timestep_weight[0], preferred_element_type=jnp.float32
    )
    kernel_body = conv_kernel[0]
    scale_row = norm_gain[0]
    shift_row = layer_norm_bias[0]
    qkv_local = qkv_weight[0]
    prompt_local = prompt_weight[0]
    out_local = out_weight[0]
    local_heads = HEADS // tile_count
    micro_ids = jnp.arange(micro_count, dtype=jnp.int32)
    prompt_all_local = jnp.einsum(
        "mtc,cjd->mtjd", prompt_tokens, prompt_local, preferred_element_type=jnp.float32
    ).astype(jnp.bfloat16)

    def prompt_for(latent_id):
        return lax.dynamic_index_in_dim(prompt_all_local, latent_id, 0, False)

    def lift_and_mix(current, temb_row):
        lifted = (current.astype(jnp.float32) + temb_row).astype(jnp.bfloat16)
        rimmed = extended(lifted, (("tile", 0),), 1)
        mixed = mix_positions(rimmed, kernel_body).reshape(token_here, width_all)
        normed = layer_norm(mixed, scale_row, shift_row).astype(jnp.bfloat16)
        return (mixed, normed)

    def section_heads(current, temb_row, prompt_pair):
        mixed, normed = lift_and_mix(current, temb_row)
        normed_all = lax.all_gather(normed, "tile", axis=0, tiled=True)
        projected = jnp.einsum(
            "tc,cjd->tjd", normed_all, qkv_local, preferred_element_type=jnp.float32
        ).astype(jnp.bfloat16)
        keys_all = jnp.concatenate([projected[:, 1], prompt_pair[:, 0]], axis=0)
        values_all = jnp.concatenate([projected[:, 2], prompt_pair[:, 1]], axis=0)
        attended = attend(projected[:, 0], keys_all, values_all, local_heads)
        update = summed_on_arrival(
            jnp.dot(attended, out_local, preferred_element_type=jnp.float32).astype(jnp.bfloat16),
            "tile",
            0,
        )
        return (mixed + update).astype(jnp.bfloat16).reshape(rows_here, cols_here, width_all)

    def advance(tick_counter, state_pair):
        carried_state, results = state_pair
        incoming = from_behind(carried_state, "section", 1)
        offset = tick_counter - section_index
        chain_level = jnp.floor_divide(offset, section_count)
        slot_index = offset - chain_level * section_count
        active = (offset >= 0) & (chain_level < chain_total) & (slot_index < micro_count)
        level_clip = jnp.clip(chain_level, 0, chain_total - 1)
        slot_clip = jnp.clip(slot_index, 0, micro_count - 1)
        noise_clip = jnp.clip(chain_level - 1, 0, chain_total - 2)
        latent_id = pick_integer(entry_order, slot_clip)
        starting = lax.dynamic_index_in_dim(latents, latent_id, 0, False)
        noise_slab = lax.dynamic_index_in_dim(
            lax.dynamic_index_in_dim(fresh_noise, noise_clip, 0, False), slot_clip, 0, False
        )
        alpha_bar = pick_scalar(alpha_table, pick_integer(timesteps, level_clip))
        renoised = (
            jnp.sqrt(alpha_bar) * incoming.astype(jnp.float32)
            + jnp.sqrt(1.0 - alpha_bar) * noise_slab.astype(jnp.float32)
        ).astype(jnp.bfloat16)
        first_section = section_index == 0
        current = jnp.where(
            first_section & (chain_level == 0),
            starting,
            jnp.where(first_section, renoised, incoming),
        )
        temb_row = lax.dynamic_index_in_dim(timestep_embedding_all, level_clip, 0, False)
        prompt_pair = prompt_for(latent_id)
        computed = section_heads(current, temb_row, prompt_pair)
        produced = jnp.where(active, computed, jnp.zeros_like(computed))
        finishing = active & (section_index == section_count - 1) & (chain_level == chain_total - 1)
        placing = finishing & (micro_ids == latent_id)
        results = jnp.where(placing[:, None, None, None], produced[None], results)
        return (produced, results)

    tick_total = chain_total * section_count + micro_count - 1
    initial_latent = (
        jnp.zeros((rows_here, cols_here, width_all), jnp.bfloat16),
        jnp.zeros_like(latents),
    )
    final_state = lax.fori_loop(0, tick_total, advance, initial_latent)
    gathered = from_root(final_state[1], "section", section_count - 1)
    share_width = width_all // section_count
    return lax.dynamic_slice_in_dim(gathered, section_index * share_width, share_width, 3)


def solution(mesh):
    placed = (
        P("batch", "tile", None, None),
        P("batch", None, None),
        P(None, "batch", "tile", None, None),
        P(),
        P("batch"),
        P("section", None, None),
        P("section", None, None),
        P("section", None),
        P("section", None),
        P("section", None, None, "tile"),
        P("section", None, None, "tile"),
        P("section", "tile", None),
    )
    return jax.shard_map(
        per_device,
        mesh=mesh,
        in_specs=placed,
        out_specs=P("batch", "tile", None, "section"),
        check_vma=False,
    )
```

profile of v0, /device:TPU:33, one launch (start us, length us, event | category | flops | bytes accessed | tf_op | source)
XLA Modules:
  0.0 1000.0 jit_solution(1695099678452104024)
XLA Ops:
  14.3 939.1 %while.18 = (s32[]{:T(128)}, bf16[1,32,1280]{2,1,0:T(8,128)(2,1)S(1)}, bf16[4,1,32,1280]{3,2,1,0:T(8,128)(2,1)}, s32[]{:T(128)}, pred[]{:T(512)}, /*index=5*/s32...) while((s32[]{:T(128)}, ...), condition=%wide.region_10.11_spmd.clone, body=%wide.region_2.10_spmd.clone.sunk | while | flops 457011904 | bytes 26369740 | solution.py:216
  36.7 10.9 %all_gather.20 = bf16[128,1280]{1,0:T(8,128)(2,1)S(1)} all-gather(bf16[32,1280]{1,0:T(8,128)(2,1)S(1)} %add_convert_fusion.5), channel_id=1, replica_groups=mesh['section'=8,'batch'=8,'tile'=4] {'tile'}, dimensions={0}, use_global_device_ids=true | all-gather | bytes 409600 | tf_op jit(solution)/shard_map/while/body/eval_jaxpr/all_gather | solution.py:162
  57.5 5.1 all-to-all-done
  64.2 4.9 collective-permute-start
  86.8 10.6 %all_gather.20 = bf16[128,1280]{1,0:T(8,128)(2,1)S(1)} all-gather(bf16[32,1280]{1,0:T(8,128)(2,1)S(1)} %add_convert_fusion.5), channel_id=1, replica_groups=mesh['section'=8,'batch'=8,'tile'=4] {'tile'}, dimensions={0}, use_global_device_ids=true | all-gather | bytes 409600 | tf_op jit(solution)/shard_map/while/body/eval_jaxpr/all_gather | solution.py:162
  107.3 5.1 all-to-all-done
  114.0 4.8 collective-permute-start
  136.5 10.4 %all_gather.20 = bf16[128,1280]{1,0:T(8,128)(2,1)S(1)} all-gather(bf16[32,1280]{1,0:T(8,128)(2,1)S(1)} %add_convert_fusion.5), channel_id=1, replica_groups=mesh['section'=8,'batch'=8,'tile'=4] {'tile'}, dimensions={0}, use_global_device_ids=true | all-gather | bytes 409600 | tf_op jit(solution)/shard_map/while/body/eval_jaxpr/all_gather | solution.py:162
  156.8 4.8 all-to-all-done
  163.3 5.3 collective-permute-start
  186.2 10.6 %all_gather.20 = bf16[128,1280]{1,0:T(8,128)(2,1)S(1)} all-gather(bf16[32,1280]{1,0:T(8,128)(2,1)S(1)} %add_convert_fusion.5), channel_id=1, replica_groups=mesh['section'=8,'batch'=8,'tile'=4] {'tile'}, dimensions={0}, use_global_device_ids=true | all-gather | bytes 409600 | tf_op jit(solution)/shard_map/while/body/eval_jaxpr/all_gather | solution.py:162
  206.7 5.3 all-to-all-done
  235.5 10.2 %all_gather.20 = bf16[128,1280]{1,0:T(8,128)(2,1)S(1)} all-gather(bf16[32,1280]{1,0:T(8,128)(2,1)S(1)} %add_convert_fusion.5), channel_id=1, replica_groups=mesh['section'=8,'batch'=8,'tile'=4] {'tile'}, dimensions={0}, use_global_device_ids=true | all-gather | bytes 409600 | tf_op jit(solution)/shard_map/while/body/eval_jaxpr/all_gather | solution.py:162
  261.7 5.2 collective-permute-start
  284.6 10.1 %all_gather.20 = bf16[128,1280]{1,0:T(8,128)(2,1)S(1)} all-gather(bf16[32,1280]{1,0:T(8,128)(2,1)S(1)} %add_convert_fusion.5), channel_id=1, replica_groups=mesh['section'=8,'batch'=8,'tile'=4] {'tile'}, dimensions={0}, use_global_device_ids=true | all-gather | bytes 409600 | tf_op jit(solution)/shard_map/while/body/eval_jaxpr/all_gather | solution.py:162
  310.8 5.8 collective-permute-start
  334.3 10.6 %all_gather.20 = bf16[128,1280]{1,0:T(8,128)(2,1)S(1)} all-gather(bf16[32,1280]{1,0:T(8,128)(2,1)S(1)} %add_convert_fusion.5), channel_id=1, replica_groups=mesh['section'=8,'batch'=8,'tile'=4] {'tile'}, dimensions={0}, use_global_device_ids=true | all-gather | bytes 409600 | tf_op jit(solution)/shard_map/while/body/eval_jaxpr/all_gather | solution.py:162
  354.8 5.3 all-to-all-done
  383.9 10.1 %all_gather.20 = bf16[128,1280]{1,0:T(8,128)(2,1)S(1)} all-gather(bf16[32,1280]{1,0:T(8,128)(2,1)S(1)} %add_convert_fusion.5), channel_id=1, replica_groups=mesh['section'=8,'batch'=8,'tile'=4] {'tile'}, dimensions={0}, use_global_device_ids=true | all-gather | bytes 409600 | tf_op jit(solution)/shard_map/while/body/eval_jaxpr/all_gather | solution.py:162
  403.9 4.6 all-to-all-done
  410.1 5.3 collective-permute-start
  433.1 10.1 %all_gather.20 = bf16[128,1280]{1,0:T(8,128)(2,1)S(1)} all-gather(bf16[32,1280]{1,0:T(8,128)(2,1)S(1)} %add_convert_fusion.5), channel_id=1, replica_groups=mesh['section'=8,'batch'=8,'tile'=4] {'tile'}, dimensions={0}, use_global_device_ids=true | all-gather | bytes 409600 | tf_op jit(solution)/shard_map/while/body/eval_jaxpr/all_gather | solution.py:162
  453.1 4.6 all-to-all-done
  459.3 5.4 collective-permute-start
  482.3 10.6 %all_gather.20 = bf16[128,1280]{1,0:T(8,128)(2,1)S(1)} all-gather(bf16[32,1280]{1,0:T(8,128)(2,1)S(1)} %add_convert_fusion.5), channel_id=1, replica_groups=mesh['section'=8,'batch'=8,'tile'=4] {'tile'}, dimensions={0}, use_global_device_ids=true | all-gather | bytes 409600 | tf_op jit(solution)/shard_map/while/body/eval_jaxpr/all_gather | solution.py:162
  502.9 4.9 all-to-all-done
  531.4 10.5 %all_gather.20 = bf16[128,1280]{1,0:T(8,128)(2,1)S(1)} all-gather(bf16[32,1280]{1,0:T(8,128)(2,1)S(1)} %add_convert_fusion.5), channel_id=1, replica_groups=mesh['section'=8,'batch'=8,'tile'=4] {'tile'}, dimensions={0}, use_global_device_ids=true | all-gather | bytes 409600 | tf_op jit(solution)/shard_map/while/body/eval_jaxpr/all_gather | solution.py:162
  558.0 5.3 collective-permute-start
  581.1 10.1 %all_gather.20 = bf16[128,1280]{1,0:T(8,128)(2,1)S(1)} all-gather(bf16[32,1280]{1,0:T(8,128)(2,1)S(1)} %add_convert_fusion.5), channel_id=1, replica_groups=mesh['section'=8,'batch'=8,'tile'=4] {'tile'}, dimensions={0}, use_global_device_ids=true | all-gather | bytes 409600 | tf_op jit(solution)/shard_map/while/body/eval_jaxpr/all_gather | solution.py:162
  601.1 4.6 all-to-all-done
  607.3 5.2 collective-permute-start
  630.1 10.0 all_gather.20
  656.2 6.1 collective-permute-start
  680.1 10.2 %all_gather.20 = bf16[128,1280]{1,0:T(8,128)(2,1)S(1)} all-gather(bf16[32,1280]{1,0:T(8,128)(2,1)S(1)} %add_convert_fusion.5), channel_id=1, replica_groups=mesh['section'=8,'batch'=8,'tile'=4] {'tile'}, dimensions={0}, use_global_device_ids=true | all-gather | bytes 409600 | tf_op jit(solution)/shard_map/while/body/eval_jaxpr/all_gather | solution.py:162
  700.2 5.4 all-to-all-done
  729.2 10.1 %all_gather.20 = bf16[128,1280]{1,0:T(8,128)(2,1)S(1)} all-gather(bf16[32,1280]{1,0:T(8,128)(2,1)S(1)} %add_convert_fusion.5), channel_id=1, replica_groups=mesh['section'=8,'batch'=8,'tile'=4] {'tile'}, dimensions={0}, use_global_device_ids=true | all-gather | bytes 409600 | tf_op jit(solution)/shard_map/while/body/eval_jaxpr/all_gather | solution.py:162
  749.3 4.6 all-to-all-done
  755.4 5.2 collective-permute-start
  778.3 10.0 all_gather.20
  804.4 5.4 collective-permute-start
  827.5 10.1 %all_gather.20 = bf16[128,1280]{1,0:T(8,128)(2,1)S(1)} all-gather(bf16[32,1280]{1,0:T(8,128)(2,1)S(1)} %add_convert_fusion.5), channel_id=1, replica_groups=mesh['section'=8,'batch'=8,'tile'=4] {'tile'}, dimensions={0}, use_global_device_ids=true | all-gather | bytes 409600 | tf_op jit(solution)/shard_map/while/body/eval_jaxpr/all_gather | solution.py:162
  853.7 5.9 collective-permute-start
  877.3 10.1 %all_gather.20 = bf16[128,1280]{1,0:T(8,128)(2,1)S(1)} all-gather(bf16[32,1280]{1,0:T(8,128)(2,1)S(1)} %add_convert_fusion.5), channel_id=1, replica_groups=mesh['section'=8,'batch'=8,'tile'=4] {'tile'}, dimensions={0}, use_global_device_ids=true | all-gather | bytes 409600 | tf_op jit(solution)/shard_map/while/body/eval_jaxpr/all_gather | solution.py:162
  897.4 5.2 all-to-all-done
  904.2 4.7 collective-permute-start
  926.5 10.5 %all_gather.20 = bf16[128,1280]{1,0:T(8,128)(2,1)S(1)} all-gather(bf16[32,1280]{1,0:T(8,128)(2,1)S(1)} %add_convert_fusion.5), channel_id=1, replica_groups=mesh['section'=8,'batch'=8,'tile'=4] {'tile'}, dimensions={0}, use_global_device_ids=true | all-gather | bytes 409600 | tf_op jit(solution)/shard_map/while/body/eval_jaxpr/all_gather | solution.py:162
  947.0 4.9 all-to-all-done
  953.5 37.9 %all-gather.3.cloned.1.call-done = bf16[32,1,32,1280]{3,2,1,0:T(8,128)(2,1)} async-done(((bf16[4,1,32,1280]{3,2,1,0:T(8,128)(2,1)}), bf16[32,1,32,1280]{3,2,1,0:T(8,128)(2,1)}) %all-gather.3.cloned.1.call-update) | async-done | bytes 2621456 | tf_op jit(solution)/shard_map/all_gather | solution.py:46
  (780 shorter events, 547.3 us)
Async XLA Ops:
  6.5 984.9 %all-gather.3.cloned.1.call-start = ((), (), s32[]{:S(2)}) async-start(), calls=%async_computation.1 | async-start | bytes 2949120 | tf_op jit(solution)/shard_map/all_gather | solution.py:46
  14.4 12.1 %collective-permute-start = (bf16[1,32,1280]{2,1,0:T(8,128)(2,1)S(1)}, bf16[1,32,1280]{2,1,0:T(8,128)(2,1)S(1)}, u32[]{:S(2)}, u32[]{:S(2)}) collective-permute-start(bf16[1,32,1280]{2,1,0:T(8,128)(2,1)S(1)} %broadcast_select_fusion.2), channel_id=1, source_target_pairs={{0,32},{32,64},{64,96},{96,128},{128,160},{160,192},{192,224},{224... | collective-permute-start | bytes 245768 | tf_op jit(solution)/shard_map/while/body/eval_jaxpr/ppermute | solution.py:42
  27.6 5.9 collective-permute-start.2
  30.9 5.2 collective-permute-start.1
  52.7 9.8 all-to-all-start
  64.2 13.4 %collective-permute-start = (bf16[1,32,1280]{2,1,0:T(8,128)(2,1)S(1)}, bf16[1,32,1280]{2,1,0:T(8,128)(2,1)S(1)}, u32[]{:S(2)}, u32[]{:S(2)}) collective-permute-start(bf16[1,32,1280]{2,1,0:T(8,128)(2,1)S(1)} %broadcast_select_fusion.2), channel_id=1, source_target_pairs={{0,32},{32,64},{64,96},{96,128},{128,160},{160,192},{192,224},{224... | collective-permute-start | bytes 245768 | tf_op jit(solution)/shard_map/while/body/eval_jaxpr/ppermute | solution.py:42
  80.9 5.2 collective-permute-start.1
  102.5 9.9 all-to-all-start
  114.0 13.3 %collective-permute-start = (bf16[1,32,1280]{2,1,0:T(8,128)(2,1)S(1)}, bf16[1,32,1280]{2,1,0:T(8,128)(2,1)S(1)}, u32[]{:S(2)}, u32[]{:S(2)}) collective-permute-start(bf16[1,32,1280]{2,1,0:T(8,128)(2,1)S(1)} %broadcast_select_fusion.2), channel_id=1, source_target_pairs={{0,32},{32,64},{64,96},{96,128},{128,160},{160,192},{192,224},{224... | collective-permute-start | bytes 245768 | tf_op jit(solution)/shard_map/while/body/eval_jaxpr/ppermute | solution.py:42
  130.6 5.2 collective-permute-start.1
  152.1 9.6 all-to-all-start
  163.3 13.8 %collective-permute-start = (bf16[1,32,1280]{2,1,0:T(8,128)(2,1)S(1)}, bf16[1,32,1280]{2,1,0:T(8,128)(2,1)S(1)}, u32[]{:S(2)}, u32[]{:S(2)}) collective-permute-start(bf16[1,32,1280]{2,1,0:T(8,128)(2,1)S(1)} %broadcast_select_fusion.2), channel_id=1, source_target_pairs={{0,32},{32,64},{64,96},{96,128},{128,160},{160,192},{192,224},{224... | collective-permute-start | bytes 245768 | tf_op jit(solution)/shard_map/while/body/eval_jaxpr/ppermute | solution.py:42
  180.4 5.2 collective-permute-start.1
  202.0 10.0 %all-to-all-start = ((bf16[4,32,1280]{2,1,0:T(8,128)(2,1)}), bf16[4,32,1280]{2,1,0:T(8,128)(2,1)S(1)}, u32[]{:S(2)}, u32[]{:S(2)}) async-start(bf16[4,32,1280]{2,1,0:T(8,128)(2,1)} %bitcast.100), calls=%async_computation | async-start | bytes 655360 | tf_op jit(solution)/shard_map/while/body/eval_jaxpr/all_to_all | solution.py:36
  213.6 12.7 %collective-permute-start = (bf16[1,32,1280]{2,1,0:T(8,128)(2,1)S(1)}, bf16[1,32,1280]{2,1,0:T(8,128)(2,1)S(1)}, u32[]{:S(2)}, u32[]{:S(2)}) collective-permute-start(bf16[1,32,1280]{2,1,0:T(8,128)(2,1)S(1)} %broadcast_select_fusion.2), channel_id=1, source_target_pairs={{0,32},{32,64},{64,96},{96,128},{128,160},{160,192},{192,224},{224... | collective-permute-start | bytes 245768 | tf_op jit(solution)/shard_map/while/body/eval_jaxpr/ppermute | solution.py:42
  229.6 5.2 collective-permute-start.1
  250.8 9.3 all-to-all-start
  261.7 13.7 %collective-permute-start = (bf16[1,32,1280]{2,1,0:T(8,128)(2,1)S(1)}, bf16[1,32,1280]{2,1,0:T(8,128)(2,1)S(1)}, u32[]{:S(2)}, u32[]{:S(2)}) collective-permute-start(bf16[1,32,1280]{2,1,0:T(8,128)(2,1)S(1)} %broadcast_select_fusion.2), channel_id=1, source_target_pairs={{0,32},{32,64},{64,96},{96,128},{128,160},{160,192},{192,224},{224... | collective-permute-start | bytes 245768 | tf_op jit(solution)/shard_map/while/body/eval_jaxpr/ppermute | solution.py:42
  299.9 9.3 all-to-all-start
  310.8 14.2 %collective-permute-start = (bf16[1,32,1280]{2,1,0:T(8,128)(2,1)S(1)}, bf16[1,32,1280]{2,1,0:T(8,128)(2,1)S(1)}, u32[]{:S(2)}, u32[]{:S(2)}) collective-permute-start(bf16[1,32,1280]{2,1,0:T(8,128)(2,1)S(1)} %broadcast_select_fusion.2), channel_id=1, source_target_pairs={{0,32},{32,64},{64,96},{96,128},{128,160},{160,192},{192,224},{224... | collective-permute-start | bytes 245768 | tf_op jit(solution)/shard_map/while/body/eval_jaxpr/ppermute | solution.py:42
  350.1 10.1 %all-to-all-start = ((bf16[4,32,1280]{2,1,0:T(8,128)(2,1)}), bf16[4,32,1280]{2,1,0:T(8,128)(2,1)S(1)}, u32[]{:S(2)}, u32[]{:S(2)}) async-start(bf16[4,32,1280]{2,1,0:T(8,128)(2,1)} %bitcast.100), calls=%async_computation | async-start | bytes 655360 | tf_op jit(solution)/shard_map/while/body/eval_jaxpr/all_to_all | solution.py:36
  361.7 12.9 %collective-permute-start = (bf16[1,32,1280]{2,1,0:T(8,128)(2,1)S(1)}, bf16[1,32,1280]{2,1,0:T(8,128)(2,1)S(1)}, u32[]{:S(2)}, u32[]{:S(2)}) collective-permute-start(bf16[1,32,1280]{2,1,0:T(8,128)(2,1)S(1)} %broadcast_select_fusion.2), channel_id=1, source_target_pairs={{0,32},{32,64},{64,96},{96,128},{128,160},{160,192},{192,224},{224... | collective-permute-start | bytes 245768 | tf_op jit(solution)/shard_map/while/body/eval_jaxpr/ppermute | solution.py:42
  378.0 5.2 collective-permute-start.1
  399.2 9.3 all-to-all-start
  410.1 13.8 %collective-permute-start = (bf16[1,32,1280]{2,1,0:T(8,128)(2,1)S(1)}, bf16[1,32,1280]{2,1,0:T(8,128)(2,1)S(1)}, u32[]{:S(2)}, u32[]{:S(2)}) collective-permute-start(bf16[1,32,1280]{2,1,0:T(8,128)(2,1)S(1)} %broadcast_select_fusion.2), channel_id=1, source_target_pairs={{0,32},{32,64},{64,96},{96,128},{128,160},{160,192},{192,224},{224... | collective-permute-start | bytes 245768 | tf_op jit(solution)/shard_map/while/body/eval_jaxpr/ppermute | solution.py:42
  427.2 5.2 collective-permute-start.1
  448.3 9.3 all-to-all-start
  459.3 13.9 %collective-permute-start = (bf16[1,32,1280]{2,1,0:T(8,128)(2,1)S(1)}, bf16[1,32,1280]{2,1,0:T(8,128)(2,1)S(1)}, u32[]{:S(2)}, u32[]{:S(2)}) collective-permute-start(bf16[1,32,1280]{2,1,0:T(8,128)(2,1)S(1)} %broadcast_select_fusion.2), channel_id=1, source_target_pairs={{0,32},{32,64},{64,96},{96,128},{128,160},{160,192},{192,224},{224... | collective-permute-start | bytes 245768 | tf_op jit(solution)/shard_map/while/body/eval_jaxpr/ppermute | solution.py:42
  498.1 9.7 all-to-all-start
  509.4 12.8 %collective-permute-start = (bf16[1,32,1280]{2,1,0:T(8,128)(2,1)S(1)}, bf16[1,32,1280]{2,1,0:T(8,128)(2,1)S(1)}, u32[]{:S(2)}, u32[]{:S(2)}) collective-permute-start(bf16[1,32,1280]{2,1,0:T(8,128)(2,1)S(1)} %broadcast_select_fusion.2), channel_id=1, source_target_pairs={{0,32},{32,64},{64,96},{96,128},{128,160},{160,192},{192,224},{224... | collective-permute-start | bytes 245768 | tf_op jit(solution)/shard_map/while/body/eval_jaxpr/ppermute | solution.py:42
  547.1 9.3 all-to-all-start
  558.0 13.8 %collective-permute-start = (bf16[1,32,1280]{2,1,0:T(8,128)(2,1)S(1)}, bf16[1,32,1280]{2,1,0:T(8,128)(2,1)S(1)}, u32[]{:S(2)}, u32[]{:S(2)}) collective-permute-start(bf16[1,32,1280]{2,1,0:T(8,128)(2,1)S(1)} %broadcast_select_fusion.2), channel_id=1, source_target_pairs={{0,32},{32,64},{64,96},{96,128},{128,160},{160,192},{192,224},{224... | collective-permute-start | bytes 245768 | tf_op jit(solution)/shard_map/while/body/eval_jaxpr/ppermute | solution.py:42
  596.4 9.3 all-to-all-start
  607.3 13.7 %collective-permute-start = (bf16[1,32,1280]{2,1,0:T(8,128)(2,1)S(1)}, bf16[1,32,1280]{2,1,0:T(8,128)(2,1)S(1)}, u32[]{:S(2)}, u32[]{:S(2)}) collective-permute-start(bf16[1,32,1280]{2,1,0:T(8,128)(2,1)S(1)} %broadcast_select_fusion.2), channel_id=1, source_target_pairs={{0,32},{32,64},{64,96},{96,128},{128,160},{160,192},{192,224},{224... | collective-permute-start | bytes 245768 | tf_op jit(solution)/shard_map/while/body/eval_jaxpr/ppermute | solution.py:42
  645.3 9.3 all-to-all-start
  656.2 14.6 %collective-permute-start = (bf16[1,32,1280]{2,1,0:T(8,128)(2,1)S(1)}, bf16[1,32,1280]{2,1,0:T(8,128)(2,1)S(1)}, u32[]{:S(2)}, u32[]{:S(2)}) collective-permute-start(bf16[1,32,1280]{2,1,0:T(8,128)(2,1)S(1)} %broadcast_select_fusion.2), channel_id=1, source_target_pairs={{0,32},{32,64},{64,96},{96,128},{128,160},{160,192},{192,224},{224... | collective-permute-start | bytes 245768 | tf_op jit(solution)/shard_map/while/body/eval_jaxpr/ppermute | solution.py:42
  695.5 10.2 %all-to-all-start = ((bf16[4,32,1280]{2,1,0:T(8,128)(2,1)}), bf16[4,32,1280]{2,1,0:T(8,128)(2,1)S(1)}, u32[]{:S(2)}, u32[]{:S(2)}) async-start(bf16[4,32,1280]{2,1,0:T(8,128)(2,1)} %bitcast.100), calls=%async_computation | async-start | bytes 655360 | tf_op jit(solution)/shard_map/while/body/eval_jaxpr/all_to_all | solution.py:36
  707.2 12.8 %collective-permute-start = (bf16[1,32,1280]{2,1,0:T(8,128)(2,1)S(1)}, bf16[1,32,1280]{2,1,0:T(8,128)(2,1)S(1)}, u32[]{:S(2)}, u32[]{:S(2)}) collective-permute-start(bf16[1,32,1280]{2,1,0:T(8,128)(2,1)S(1)} %broadcast_select_fusion.2), channel_id=1, source_target_pairs={{0,32},{32,64},{64,96},{96,128},{128,160},{160,192},{192,224},{224... | collective-permute-start | bytes 245768 | tf_op jit(solution)/shard_map/while/body/eval_jaxpr/ppermute | solution.py:42
  723.4 5.2 collective-permute-start.1
  744.5 9.3 all-to-all-start
  755.4 13.7 %collective-permute-start = (bf16[1,32,1280]{2,1,0:T(8,128)(2,1)S(1)}, bf16[1,32,1280]{2,1,0:T(8,128)(2,1)S(1)}, u32[]{:S(2)}, u32[]{:S(2)}) collective-permute-start(bf16[1,32,1280]{2,1,0:T(8,128)(2,1)S(1)} %broadcast_select_fusion.2), channel_id=1, source_target_pairs={{0,32},{32,64},{64,96},{96,128},{128,160},{160,192},{192,224},{224... | collective-permute-start | bytes 245768 | tf_op jit(solution)/shard_map/while/body/eval_jaxpr/ppermute | solution.py:42
  793.5 9.3 all-to-all-start
  804.4 13.9 %collective-permute-start = (bf16[1,32,1280]{2,1,0:T(8,128)(2,1)S(1)}, bf16[1,32,1280]{2,1,0:T(8,128)(2,1)S(1)}, u32[]{:S(2)}, u32[]{:S(2)}) collective-permute-start(bf16[1,32,1280]{2,1,0:T(8,128)(2,1)S(1)} %broadcast_select_fusion.2), channel_id=1, source_target_pairs={{0,32},{32,64},{64,96},{96,128},{128,160},{160,192},{192,224},{224... | collective-permute-start | bytes 245768 | tf_op jit(solution)/shard_map/while/body/eval_jaxpr/ppermute | solution.py:42
  842.8 9.3 all-to-all-start
  853.7 14.4 %collective-permute-start = (bf16[1,32,1280]{2,1,0:T(8,128)(2,1)S(1)}, bf16[1,32,1280]{2,1,0:T(8,128)(2,1)S(1)}, u32[]{:S(2)}, u32[]{:S(2)}) collective-permute-start(bf16[1,32,1280]{2,1,0:T(8,128)(2,1)S(1)} %broadcast_select_fusion.2), channel_id=1, source_target_pairs={{0,32},{32,64},{64,96},{96,128},{128,160},{160,192},{192,224},{224... | collective-permute-start | bytes 245768 | tf_op jit(solution)/shard_map/while/body/eval_jaxpr/ppermute | solution.py:42
  892.6 10.0 all-to-all-start
  904.2 13.2 %collective-permute-start = (bf16[1,32,1280]{2,1,0:T(8,128)(2,1)S(1)}, bf16[1,32,1280]{2,1,0:T(8,128)(2,1)S(1)}, u32[]{:S(2)}, u32[]{:S(2)}) collective-permute-start(bf16[1,32,1280]{2,1,0:T(8,128)(2,1)S(1)} %broadcast_select_fusion.2), channel_id=1, source_target_pairs={{0,32},{32,64},{64,96},{96,128},{128,160},{160,192},{192,224},{224... | collective-permute-start | bytes 245768 | tf_op jit(solution)/shard_map/while/body/eval_jaxpr/ppermute | solution.py:42
  942.3 9.6 all-to-all-start
  (90 other events, 775.3 us)
Sparse Core Ops, SparseCore 0:
  953.6 37.7 all-gather.2
where the time goes:
time: 1010 us; the launch traced here: 1000 us
  starting transfers between devices  228 us (23%)
  blocking collectives  196 us (19%)
  waiting for transfers between devices  177 us (18%)
  other arithmetic  151 us (15%)
  matrix products  90.6 us (9%)
  local copies, waits for them, and re-layouts  77.4 us (8%)
  loops' own time  66.7 us (7%)
  between operations  13.5 us (1%)
    all_gather x19, blocking collectives, section_heads(): normed_all = lax.all_gather(normed, 'tile', axis=0, tiled=True)  196 us
    ppermute x19, starting transfers between devices, from_behind(): lax.ppermute(shard, axis, [(i, (i + by) % count) for i in range(count)])  95.3 us
    all_to_all x19, waiting for transfers between devices, summed_on_arrival(): lax.all_to_all(parts, axis, split_axis=0, concat_axis=0, tiled=True)  92 us
    another operation x1, loops' own time, per_device(): final_state = lax.fori_loop(0, tick_total, advance, initial_latent)  66.7 us
    all_to_all x19, starting transfers between devices, summed_on_arrival(): lax.all_to_all(parts, axis, split_axis=0, concat_axis=0, tiled=True)  65.6 us
    reduce_sum x38, other arithmetic, pick_integer(): return jnp.sum(jnp.where(hits, int_table, jnp.zeros_like(int_table)))  50.8 us
    ppermute x19, waiting for transfers between devices, extended(): lax.ppermute(head, axis, [((i + 1) % count, i) for i in range(ends)])  47.1 us
    dot_general x19, matrix products, section_heads(): jnp.dot(attended, out_local, preferred_element_type=jnp.float32)  43.2 us
  transfers between devices with their start and end apart: 77, of which 39 were waited for; matrix products, arithmetic and copies ran while one was open for 15% of the time, Pallas kernels for 0%

commit v1 on v0

v1 whole, which is shorter than its diff:
```python
import functools
import math

import jax
import jax.numpy as jnp
from jax import lax
from jax.experimental import pallas as pl
from jax.experimental.pallas import tpu as pltpu
from jax.sharding import PartitionSpec as P

MESH = pl.DeviceIdType.MESH
F32 = jnp.float32
BF16 = jnp.bfloat16
WIDTH = 1280
HALF = 640
TOKENS = 128
TEXT = 77
TEXT_PAD = 80


def kernel(
    layers_z,
    order,
    steps,
    latents,
    noise,
    ptok,
    tweight,
    conv,
    gain,
    bias,
    wcat,
    wout,
    wprompt,
    out,
    wq,
    wo,
    ptok_v,
    wp_v,
    tw_v,
    pk_f,
    pk_s,
    pk_v,
    par,
    xin,
    nz,
    nsend,
    xc,
    mixed,
    normed,
    qkv,
    att,
    part_s,
    part_r,
    xs,
    fin,
    wr_sem,
    ws_sem,
    wrel_sem,
    own_l_sem,
    own_s_sem,
    own_r_sem,
    xa_s_sem,
    xa_r_sem,
    xa_l_sem,
    nz_s_sem,
    nz_r_sem,
    ld_sem,
    par_s_sem,
    par_r_sem,
    pk_s_sem,
    pk_r_sem,
    hop_s_sem,
    hop_r_sem,
    rel_s_sem,
    rel_r_sem,
    pt_s_sem,
    pt_r_sem,
    out_s_sem,
    out_r_sem,
):
    s = lax.axis_index("section")
    b = lax.axis_index("batch")
    t = lax.axis_index("tile")
    batches = lax.axis_size("batch")
    zh = s // 2
    c = s % 2
    oc = 1 - c
    p = (b // layers_z) % 2
    t_pair = t // 2
    t_low = t % 2
    is_own = c == t_pair
    b_up = lax.rem(b + layers_z, batches)
    b_down = lax.rem(b + batches - layers_z, batches)
    jd = 1 - t_low
    jf = t_low
    y_d = 2 * c + jd
    from_below = lax.rem(y_d + 1, 4) == t
    e_rel = jnp.where(from_below, 0, 1)
    t_rel = jnp.where(from_below, lax.rem(t + 1, 4), lax.rem(t + 3, 4))
    first = zh == 0
    last = zh == 3

    def remote(src, dst, ssem, rsem, **where):
        return pltpu.make_async_remote_copy(
            src_ref=src, dst_ref=dst, send_sem=ssem, recv_sem=rsem, device_id=where, device_id_type=MESH
        )

    def rows(start, size, unit):
        return pl.ds(pl.multiple_of(start, unit), size)

    barrier = pltpu.get_barrier_semaphore()

    def greet(n, _):
        s2 = n // 4
        t2 = n % 4

        @pl.when(jnp.logical_or(s2 != s, t2 != t))
        def _():
            pl.semaphore_signal(barrier, inc=1, device_id={"section": s2, "tile": t2}, device_id_type=MESH)

        return 0

    lax.fori_loop(0, 32, greet, 0)
    for b2 in (b_up, b_down):
        pl.semaphore_signal(barrier, inc=1, device_id={"batch": b2}, device_id_type=MESH)

    load_tok = pltpu.make_async_copy(ptok, ptok_v, ld_sem.at[0])
    load_wp = pltpu.make_async_copy(wprompt, wp_v, ld_sem.at[1])
    load_tw = pltpu.make_async_copy(tweight, tw_v, ld_sem.at[2])
    load_tw.start()
    load_tok.start()
    load_wp.start()

    pl.semaphore_wait(barrier, 33)

    def latent_copy(d, h):
        t2 = lax.rem(t + d, 4)
        return remote(
            latents.at[t2, :, pl.ds(HALF * h, HALF)],
            xin.at[0, h, rows(32 * t, 32, 32), :],
            xa_s_sem.at[d - 1, h],
            xa_r_sem.at[d - 1, h],
            tile=t2,
        )

    def latent_local(h):
        return pltpu.make_async_copy(
            latents.at[t, :, pl.ds(HALF * h, HALF)], xin.at[0, h, rows(32 * t, 32, 32), :], xa_l_sem.at[h]
        )

    @pl.when(first)
    def _():
        for d in (1, 3, 2):
            for h in range(2):
                latent_copy(d, h).start()
        for h in range(2):
            latent_local(h).start()

    def quarter(arr, q):
        return rows(320 * q, 320, 320) if arr == 0 else rows(80 * q, 80, 80)

    gathered = (wq, wo)
    sources = (wcat, wout)

    def direct_copy(arr, way, e):
        t2 = lax.rem(t + (1, 3)[way], 4)
        q = 2 * p + e
        return remote(
            sources[arr].at[quarter(arr, q), :],
            gathered[arr].at[c, t_low, quarter(arr, q), :],
            ws_sem.at[arr, way, e],
            wr_sem.at[arr, c, t_low, q],
            section=2 * zh + t_pair,
            tile=t2,
        )

    for arr in range(2):
        for e in range(2):
            for way in range(2):
                direct_copy(arr, way, (e + way) % 2).start()

    def own_local(arr):
        return pltpu.make_async_copy(sources[arr], gathered[arr].at[c, t_low], own_l_sem.at[arr])

    def own_remote(arr):
        return remote(
            sources[arr], gathered[arr].at[c, t_low], own_s_sem.at[arr], own_r_sem.at[arr], section=2 * zh + oc
        )

    def own_arrival(arr):
        return remote(
            sources[arr], gathered[arr].at[oc, t_low], own_s_sem.at[arr], own_r_sem.at[arr], section=2 * zh + oc
        )

    @pl.when(is_own)
    def _():
        for arr in range(2):
            own_local(arr).start()

    @pl.when(jnp.logical_not(is_own))
    def _():
        for arr in range(2):
            own_remote(arr).start()

    def noise_copy(d):
        t2 = lax.rem(t + d, 4)
        return remote(nsend.at[t2], nz.at[t], nz_s_sem.at[d - 1], nz_r_sem.at[d - 1], tile=t2)

    @pl.when(first)
    def _():
        for t2 in range(4):
            at = jnp.int32(0)
            for m in range(4):
                at = jnp.where(order[m] == t2, m, at)
            nsend[t2] = noise[at]
        for d in (1, 3, 2):
            noise_copy(d).start()
        nz[t] = nsend[t]

    par[c, 0:9, :] = conv[...]
    par[c, 9:10, :] = gain[...]
    par[c, 10:11, :] = bias[...]
    lane = lax.broadcasted_iota(jnp.int32, (16, 320), 1)
    row = lax.broadcasted_iota(jnp.int32, (16, 320), 0)
    spot = jnp.where(lane < 160, lane, lane - 160).astype(F32)
    freq = jnp.exp(-math.log(10000.0) * (spot / 160.0))
    moment = jnp.where(row == 0, steps[0].astype(F32), steps[1].astype(F32))
    angle = moment * freq
    feats = jnp.where(lane < 160, jnp.cos(angle), jnp.sin(angle)).astype(BF16)
    load_tw.wait()
    temb_all = jnp.dot(feats, tw_v[...], preferred_element_type=F32)
    par[c, 11:13, :] = temb_all[0:2]
    par_copy = remote(par.at[c], par.at[c], par_s_sem, par_r_sem, section=2 * zh + oc)
    par_copy.start()

    spots = (
        lax.broadcasted_iota(jnp.int32, (8, 128), 0) * 128 + lax.broadcasted_iota(jnp.int32, (8, 128), 1)
    )
    low_root = math.sqrt(0.00085)
    high_root = math.sqrt(0.012)
    roots = low_root + (high_root - low_root) * spots.astype(F32) / 999.0
    logs = jnp.where(spots <= steps[1], jnp.log(1.0 - roots * roots), 0.0)
    total = jnp.sum(jnp.sum(logs, axis=0, keepdims=True), axis=1, keepdims=True)
    alpha_bar = jnp.exp(total)
    keep = jnp.sqrt(alpha_bar)
    fresh = jnp.sqrt(1.0 - alpha_bar)

    pk_f[72:80, :] = jnp.zeros((8, HALF), F32)
    for i in range(2):
        for j in range(2):
            pk_v[i, j, TEXT_PAD:, :] = jnp.zeros((TOKENS - TEXT_PAD, HALF), BF16)
    load_tok.wait()
    load_wp.wait()

    def pk_copy(tt):
        return remote(
            pk_s.at[tt],
            pk_v.at[c, t_low, 0:TEXT_PAD, :],
            pk_s_sem.at[tt],
            pk_r_sem.at[c, t_low],
            section=2 * zh + t_pair,
            tile=tt,
        )

    def pk_is_self(tt):
        return jnp.logical_and(tt == t, is_own)

    def prompt_one(tt, _):
        pk_f[0:TEXT, :] = jnp.dot(ptok_v[tt], wp_v[...], preferred_element_type=F32)
        pk_s[tt] = pk_f[...].astype(BF16)

        @pl.when(jnp.logical_not(pk_is_self(tt)))
        def _():
            pk_copy(tt).start()

        @pl.when(pk_is_self(tt))
        def _():
            pk_v[c, t_low, 0:TEXT_PAD, :] = pk_s[tt]

        return 0

    lax.fori_loop(0, 4, prompt_one, 0)

    @pl.when(is_own)
    def _():
        for arr in range(2):
            own_local(arr).wait()
            own_arrival(arr).wait_recv()

    @pl.when(jnp.logical_not(is_own))
    def _():
        for arr in range(2):
            own_remote(arr).wait_send()

    def piece(arr, i, j, q):
        return gathered[arr].at[i, j, quarter(arr, q), :]

    def hand_on(arr, i, j, q, ssem, **where):
        return remote(piece(arr, i, j, q), piece(arr, i, j, q), ssem, wr_sem.at[arr, i, j, q], **where)

    def row_relay(arr, i):
        return hand_on(arr, i, jd, 2 * p + e_rel, wrel_sem.at[arr, i, 0], tile=t_rel)

    def side_relay(arr, i, j, e, slot):
        return hand_on(arr, i, j, 2 * p + e, wrel_sem.at[arr, i, slot], batch=(b_up, b_down)[e])

    def arrived(arr, i, j, q):
        hand_on(arr, i, j, q, wrel_sem.at[arr, i, 0], tile=t_rel).wait_recv()

    def relay(i, _):
        for arr in range(2):
            arrived(arr, i, jd, 2 * p + e_rel)
            row_relay(arr, i).start()
            arrived(arr, i, jd, 2 * p + 1 - e_rel)
            for e in range(2):
                side_relay(arr, i, jd, e, 1 + e).start()

        @pl.when(jnp.logical_not(is_own))
        def _():
            for arr in range(2):
                for e in range(2):
                    arrived(arr, i, jf, 2 * p + e)
                    side_relay(arr, i, jf, e, 3 + e).start()

        return 0

    lax.fori_loop(0, 2, relay, 0)

    par_arrival = remote(par.at[oc], par.at[oc], par_s_sem, par_r_sem, section=2 * zh + oc)
    par_arrival.wait_recv()

    def others(arr, i):
        for e in range(2):
            arrived(arr, i, jd, 2 * (1 - p) + e)

        @pl.when(jnp.logical_not(is_own))
        def _():
            for e in range(2):
                arrived(arr, i, jf, 2 * (1 - p) + e)

    def hop_copy(k, k_to):
        return remote(
            xs.at[k], xin.at[k_to, c], hop_s_sem.at[k], hop_r_sem.at[k_to], section=lax.rem(s + 2, 8)
        )

    def half_relay(k):
        return remote(xin.at[k, c], xin.at[k, c], rel_s_sem.at[k], rel_r_sem.at[k], section=2 * zh + oc)

    def half_arrival(k):
        return remote(xin.at[k, oc], xin.at[k, oc], rel_s_sem.at[k], rel_r_sem.at[k], section=2 * zh + oc)

    def part_copy(n, g):
        return remote(part_s.at[n, g], part_r.at[n, g], pt_s_sem.at[n, g], pt_r_sem.at[n, g], section=2 * zh + oc)

    def out_copy(q, t2):
        return remote(
            fin.at[q, rows(32 * t2, 32, 32), :],
            out.at[t],
            out_s_sem.at[q, t2],
            out_r_sem.at[t],
            section=4 * c + q,
            tile=t2,
        )

    column = lax.broadcasted_iota(jnp.int32, (TOKENS, 128), 0) % 32
    lane_row = lax.broadcasted_iota(jnp.int32, (1, 128), 1)
    low_f = jnp.where(lane_row < 64, 1.0, 0.0)
    lo = low_f.astype(BF16)
    hi = (1.0 - low_f).astype(BF16)
    is_low = lax.broadcasted_iota(jnp.int32, (TOKENS, 128), 1) < 64
    is_text = lax.broadcasted_iota(jnp.int32, (256, 256), 1) < TOKENS + TEXT
    scale = math.log2(math.e) / 8.0

    def stage(n, _):
        k = n // 2
        i = n % 2
        at_start = jnp.logical_and(first, k == 0)

        @pl.when(jnp.logical_and(i == 0, at_start))
        def _():
            for d in (1, 2, 3):
                for h in range(2):
                    latent_copy(d, h).wait_recv()
            for h in range(2):
                latent_local(h).wait()

        @pl.when(jnp.logical_and(i == 0, jnp.logical_not(at_start)))
        def _():
            hop_copy(k, k).wait_recv()
            half_relay(k).start()
            half_arrival(k).wait_recv()

        @pl.when(jnp.logical_and(i == 0, jnp.logical_and(first, k == 1)))
        def _():
            for d in (1, 2, 3):
                noise_copy(d).wait_recv()
            for h in range(2):
                for r in range(4):
                    old = xin[1, h, 32 * r : 32 * r + 32, :].astype(F32)
                    new = nz[r, :, HALF * h : HALF * h + HALF].astype(F32)
                    xc[h, 32 * r : 32 * r + 32, :] = (keep * old + fresh * new).astype(BF16)

        @pl.when(jnp.logical_and(i == 0, jnp.logical_not(jnp.logical_and(first, k == 1))))
        def _():
            xc[...] = xin[k]

        sums = jnp.zeros((TOKENS, 128), F32)
        for h in range(2):
            for l in range(5):
                ch = slice(HALF * h + 128 * l, HALF * h + 128 * l + 128)
                here = slice(128 * l, 128 * l + 128)
                temb = jnp.where(k == 0, par[i, 11:12, ch], par[i, 12:13, ch])
                lifted = (xc[h, :, here].astype(F32) + temb).astype(BF16).astype(F32)
                before = jnp.where(column == 0, 0.0, pltpu.roll(lifted, 1, 0))
                after = jnp.where(column == 31, 0.0, pltpu.roll(lifted, TOKENS - 1, 0))
                lines = []
                for a in range(3):
                    lines.append(
                        par[i, 3 * a : 3 * a + 1, ch] * before
                        + par[i, 3 * a + 1 : 3 * a + 2, ch] * lifted
                        + par[i, 3 * a + 2 : 3 * a + 3, ch] * after
                    )
                blank = jnp.zeros((32, 128), F32)
                above = jnp.concatenate([blank, lines[0][: TOKENS - 32]], axis=0)
                below = jnp.concatenate([lines[2][32:], blank], axis=0)
                got = lifted + above + lines[1] + below
                mixed[h, :, here] = got
                sums = sums + got
        centre = jnp.sum(sums, axis=1, keepdims=True) * (1.0 / WIDTH)
        squares = jnp.zeros((TOKENS, 128), F32)
        for h in range(2):
            for l in range(5):
                off = mixed[h, :, 128 * l : 128 * l + 128] - centre
                squares = squares + off * off
        spread = jnp.sum(squares, axis=1, keepdims=True) * (1.0 / WIDTH)
        inv = lax.rsqrt(spread + 1e-05)
        for h in range(2):
            for l in range(5):
                ch = slice(HALF * h + 128 * l, HALF * h + 128 * l + 128)
                off = mixed[h, :, 128 * l : 128 * l + 128] - centre
                normed[:, ch] = (off * inv * par[i, 9:10, ch] + par[i, 10:11, ch]).astype(BF16)

        @pl.when(k == 0)
        def _():
            others(0, i)

        for j in range(2):
            for m in range(4):
                cols = slice(256 * m, 256 * m + 256)
                qkv[j, :, cols] = jnp.dot(normed[...], wq[i, j, :, cols], preferred_element_type=F32).astype(BF16)

        @pl.when(k == 0)
        def _():
            for j in range(2):
                me = jnp.logical_and(i == c, 2 * c + j == t)

                @pl.when(jnp.logical_not(me))
                def _():
                    remote(
                        pk_s.at[0],
                        pk_v.at[i, j, 0:TEXT_PAD, :],
                        pk_s_sem.at[0],
                        pk_r_sem.at[i, j],
                        section=2 * zh + oc,
                    ).wait_recv()

        def block(j, m):
            return qkv[j, :, 128 * m : 128 * m + 128]

        def text(j, m):
            return pk_v[i, j, :, 128 * m : 128 * m + 128]

        heads = []
        for j in range(2):
            heads.append((block(j, 0), block(j, 3), block(j, 5), text(j, 0), text(j, 2), False))
            heads.append((block(j, 1), block(j, 4), block(j, 6), text(j, 1), text(j, 3), False))
        heads.append(
            (
                block(0, 2) * lo + block(1, 2) * hi,
                block(0, 7) + block(1, 7),
                block(1, 2) * lo + block(0, 2) * hi,
                text(0, 4) * lo + text(1, 4) * hi,
                text(1, 4) * lo + text(0, 4) * hi,
                True,
            )
        )
        for at, (q_pair, k_self, v_self, k_text, v_text, crossed) in enumerate(heads):
            lhs = jnp.concatenate([q_pair * lo, q_pair * hi], axis=0)
            keys = jnp.concatenate([k_self, k_text], axis=0)
            vals = jnp.concatenate([v_self, v_text], axis=0)
            scores = lax.dot_general(lhs, keys, (((1,), (1,)), ((), ())), preferred_element_type=F32)
            powers = jnp.where(is_text, jnp.exp2(scores * scale), 0.0)
            inverse = 1.0 / jnp.sum(powers, axis=1, keepdims=True)
            weights = (powers * inverse).astype(BF16)
            got = jnp.dot(weights, vals, preferred_element_type=F32)
            top, bottom = got[:TOKENS], got[TOKENS:]
            pair = jnp.where(is_low, bottom, top) if crossed else jnp.where(is_low, top, bottom)
            att[:, 128 * at : 128 * at + 128] = pair.astype(BF16)

        @pl.when(k == 0)
        def _():
            others(1, i)

        def product(g):
            cols = rows(HALF * g, HALF, 128)
            mat = jnp.concatenate(
                [
                    wo[i, 0, 0:256, cols],
                    wo[i, 1, 0:256, cols],
                    wo[i, 1, 256:320, cols],
                    wo[i, 0, 256:320, cols],
                ],
                axis=0,
            )
            return jnp.dot(att[...], mat, preferred_element_type=F32).astype(BF16)

        part_s[n, oc] = product(oc)
        part_copy(n, oc).start()
        part_s[n, c] = product(c)

        @pl.when(i == 0)
        def _():
            part_copy(n, c).start()

        def added(g):
            update = part_s[n, g].astype(F32) + part_r[n, g].astype(F32)
            return (mixed[g] + update).astype(BF16)

        part_copy(n, c).wait_recv()
        mine = added(c)

        @pl.when(i == 0)
        def _():
            xc[c] = mine
            part_copy(n, oc).wait_recv()
            xc[oc] = added(oc)

        at_end = jnp.logical_and(last, k == 1)

        @pl.when(jnp.logical_and(i == 1, jnp.logical_not(at_end)))
        def _():
            xs[k] = mine
            hop_copy(k, jnp.where(last, 1, k)).start()

        @pl.when(jnp.logical_and(i == 1, at_end))
        def _():
            for q in range(4):
                fin[q] = mine[:, 160 * q : 160 * q + 160]
            for q in range(4):
                for t2 in range(4):
                    own = jnp.logical_and(s == 4 * c + q, t == t2)

                    @pl.when(jnp.logical_not(own))
                    def _():
                        out_copy(q, t2).start()

                    @pl.when(own)
                    def _():
                        out[t] = fin[q, 32 * t2 : 32 * t2 + 32, :]

        return 0

    lax.fori_loop(0, 4, stage, 0)

    for t2 in range(4):
        own = jnp.logical_and(s == 7, t == t2)

        @pl.when(jnp.logical_not(own))
        def _():
            remote(
                fin.at[0, 0:32, :], out.at[t2], out_s_sem.at[0, 0], out_r_sem.at[t2], section=2 * zh + oc
            ).wait_recv()

    @pl.when(last)
    def _():
        for q in range(4):
            for t2 in range(4):
                own = jnp.logical_and(s == 4 * c + q, t == t2)

                @pl.when(jnp.logical_not(own))
                def _():
                    out_copy(q, t2).wait_send()

    @pl.when(first)
    def _():
        for d in (1, 2, 3):
            for h in range(2):
                latent_copy(d, h).wait_send()
            noise_copy(d).wait_send()

    for arr in range(2):
        for way in range(2):
            for e in range(2):
                direct_copy(arr, way, e).wait_send()
    par_copy.wait_send()
    for tt in range(4):

        @pl.when(jnp.logical_not(pk_is_self(tt)))
        def _():
            pk_copy(tt).wait_send()

    for i in range(2):
        for arr in range(2):
            row_relay(arr, i).wait_send()
            for e in range(2):
                side_relay(arr, i, jd, e, 1 + e).wait_send()

        @pl.when(jnp.logical_not(is_own))
        def _():
            for arr in range(2):
                for e in range(2):
                    side_relay(arr, i, jf, e, 3 + e).wait_send()

    for n in range(4):
        part_copy(n, oc).wait_send()
        if n % 2 == 0:
            part_copy(n, c).wait_send()
    for k in range(2):

        @pl.when(jnp.logical_not(jnp.logical_and(first, k == 0)))
        def _():
            half_relay(k).wait_send()

        @pl.when(jnp.logical_not(jnp.logical_and(last, k == 1)))
        def _():
            hop_copy(k, jnp.where(last, 1, k)).wait_send()


def arranged(low, parts, first_odd, second_odd):
    odd = jnp.where(low == 0, jnp.concatenate([first_odd, second_odd], 1), jnp.concatenate([second_odd, first_odd], 1))
    return jnp.concatenate([*parts, odd], axis=1)


def per_device(
    layers_z,
    latents,
    prompt_tokens,
    fresh_noise,
    timesteps,
    entry_order,
    timestep_weight,
    conv_kernel,
    norm_gain,
    layer_norm_bias,
    qkv_weight,
    prompt_weight,
    out_weight,
):
    low = lax.axis_index("tile") % 2
    q, k, v = (qkv_weight[0, :, m] for m in range(3))
    blank = jnp.zeros((q.shape[0], 64), BF16)
    odd = jnp.where(low == 0, jnp.concatenate([q[:, 256:], v[:, 256:]], 1), jnp.concatenate([v[:, 256:], q[:, 256:]], 1))
    rest = jnp.where(low == 0, jnp.concatenate([k[:, 256:], blank], 1), jnp.concatenate([blank, k[:, 256:]], 1))
    wcat = jnp.concatenate([q[:, :256], odd, k[:, :256], v[:, :256], rest], axis=1)
    pk, pv = prompt_weight[0, :, 0], prompt_weight[0, :, 1]
    wprompt = arranged(low, [pk[:, :256], pv[:, :256]], pk[:, 256:], pv[:, 256:])

    vmem = pl.BlockSpec(memory_space=pltpu.VMEM)
    smem = pl.BlockSpec(memory_space=pltpu.SMEM)
    held = pl.BlockSpec(memory_space=pl.ANY)
    dma = pltpu.SemaphoreType.DMA
    micro, _, cols, width = latents.shape
    return pl.pallas_call(
        functools.partial(kernel, layers_z),
        out_shape=jax.ShapeDtypeStruct((micro, cols, width // 8), BF16),
        in_specs=[smem, smem, held, vmem, held, held, vmem, vmem, vmem, held, held, held],
        out_specs=vmem,
        scratch_shapes=[
            pltpu.VMEM((2, 2, WIDTH, 1024), BF16),
            pltpu.VMEM((2, 2, 320, WIDTH), BF16),
            pltpu.VMEM((4, TEXT, 2048), BF16),
            pltpu.VMEM((2048, HALF), BF16),
            pltpu.VMEM((320, WIDTH), BF16),
            pltpu.VMEM((TEXT_PAD, HALF), F32),
            pltpu.VMEM((4, TEXT_PAD, HALF), BF16),
            pltpu.VMEM((2, 2, TOKENS, HALF), BF16),
            pltpu.VMEM((2, 16, WIDTH), F32),
            pltpu.VMEM((2, 2, TOKENS, HALF), BF16),
            pltpu.VMEM((4, 32, WIDTH), BF16),
            pltpu.VMEM((4, 32, WIDTH), BF16),
            pltpu.VMEM((2, TOKENS, HALF), BF16),
            pltpu.VMEM((2, TOKENS, HALF), F32),
            pltpu.VMEM((TOKENS, WIDTH), BF16),
            pltpu.VMEM((2, TOKENS, 1024), BF16),
            pltpu.VMEM((TOKENS, HALF), BF16),
            pltpu.VMEM((4, 2, TOKENS, HALF), BF16),
            pltpu.VMEM((4, 2, TOKENS, HALF), BF16),
            pltpu.VMEM((2, TOKENS, HALF), BF16),
            pltpu.VMEM((4, TOKENS, 160), BF16),
            dma((2, 2, 2, 4)),
            dma((2, 2, 2)),
            dma((2, 2, 5)),
            dma((2,)),
            dma((2,)),
            dma((2,)),
            dma((3, 2)),
            dma((3, 2)),
            dma((2,)),
            dma((3,)),
            dma((3,)),
            dma((3,)),
            dma,
            dma,
            dma((4,)),
            dma((2, 2)),
            dma((2,)),
            dma((2,)),
            dma((2,)),
            dma((2,)),
            dma((4, 2)),
            dma((4, 2)),
            dma((4, 4)),
            dma((4,)),
        ],
        compiler_params=pltpu.CompilerParams(collective_id=0, has_side_effects=True),
    )(
        entry_order,
        timesteps,
        latents[:, 0],
        fresh_noise[0, :, 0],
        prompt_tokens,
        timestep_weight[0],
        conv_kernel[0],
        norm_gain,
        layer_norm_bias,
        wcat,
        out_weight[0],
        wprompt,
    )[:, None]


def solution(mesh):
    layers_z = 2 if mesh.shape["batch"] >= 4 else 1
    placed = (
        P("batch", "tile", None, None),
        P("batch", None, None),
        P(None, "batch", "tile", None, None),
        P(),
        P("batch"),
        P("section", None, None),
        P("section", None, None),
        P("section", None),
        P("section", None),
        P("section", None, None, "tile"),
        P("section", None, None, "tile"),
        P("section", "tile", None),
    )
    return jax.shard_map(
        functools.partial(per_device, layers_z),
        mesh=mesh,
        in_specs=placed,
        out_specs=P("batch", "tile", None, "section"),
        check_vma=False,
    )
```

time: 1010 us -> 258 us (0.26)
  starting transfers between devices: 228 us -> 0 us
  Pallas kernels: 0 us -> 225 us
  blocking collectives: 196 us -> 0 us
  waiting for transfers between devices: 177 us -> 0 us
  other arithmetic: 151 us -> 5.54 us
  matrix products: 90.6 us -> 0 us
  loops' own time: 66.7 us -> 0 us
  local copies, waits for them, and re-layouts: 77.4 us -> 26.6 us
  between operations: 13.5 us -> 0.1 us
    pallas_call x0 -> x1, Pallas kernels: none -> 225 us  [per_device(): pl.pallas_call(functools.partial(kernel, layers_z), out_shape=jax.ShapeDt...]
    all_gather x19 -> x0, blocking collectives: 196 us -> none  [section_heads(): normed_all = lax.all_gather(normed, 'tile', axis=0, tiled=True)]
    ppermute x57 -> x0, starting transfers between devices: 163 us -> none  [the longest x19 95.3 us: from_behind(): lax.ppermute(shard, axis, [(i, (i + by) % count) for i in range(count)])]
    all_to_all x19 -> x0, waiting for transfers between devices: 92 us -> none  [summed_on_arrival(): lax.all_to_all(parts, axis, split_axis=0, concat_axis=0, tiled=True)]
    dot_general x78 -> x0, matrix products: 90.6 us -> none  [the longest x19 43.2 us: section_heads(): jnp.dot(attended, out_local, preferred_element_type=jnp.float32)]
    reduce_sum x114 -> x0, other arithmetic: 84.8 us -> none  [the longest x38 50.8 us: pick_integer(): return jnp.sum(jnp.where(hits, int_table, jnp.zeros_like(int_table)))]
    another operation x1 -> x0, loops' own time: 66.7 us -> none  [per_device(): final_state = lax.fori_loop(0, tick_total, advance, initial_latent)]
    all_to_all x19 -> x0, starting transfers between devices: 65.6 us -> none  [summed_on_arrival(): lax.all_to_all(parts, axis, split_axis=0, concat_axis=0, tiled=True)]
  transfers between devices with their start and end apart: 77 -> 0, of which waited for: 39 -> 0; matrix products, arithmetic and copies ran while one was open for 15% -> 0% of each run, Pallas kernels for 0% -> 0%
where the time goes in v1:
time: 258 us
  Pallas kernels  225 us (87%)
  local copies, waits for them, and re-layouts  26.6 us (10%)
  other arithmetic  5.54 us (2%)
    pallas_call x1, Pallas kernels, per_device(): pl.pallas_call(functools.partial(kernel, layers_z), out_shape=jax.ShapeDt...  225 us
    unnamed x17, local copies, waits for them, and re-layouts  18.8 us

profile of v1, /device:TPU:33, one launch (start us, length us, event | category | flops | bytes accessed | tf_op | source)
XLA Modules:
  0.0 257.7 jit_solution(4375059331755313965)
XLA Ops:
  0.0 0.0 copy-start.2
  0.0 3.2 %copy.18.ptok = bf16[4,77,2048]{2,1,0:T(8,128)(2,1)} copy(bf16[4,77,2048]{2,0,1:T(4,128)(2,1)} %param.13) | data formatting | bytes 2523136 | tf_op args[1]
  3.3 1.4 copy.27
  4.7 0.0 copy-done.2
  4.7 1.1 fusion.2
  5.7 1.3 copy.21
  7.0 1.2 slice_dynamic-update-slice_fusion.2
  8.2 2.2 copy.22
  10.4 1.8 slice.65
  12.2 1.7 slice.64
  13.9 1.7 fusion
  15.6 1.3 copy.23
  17.0 0.0 copy-start.1
  17.0 1.3 slice_dynamic-update-slice_fusion.1
  18.3 1.2 slice_dynamic-update-slice_fusion
  19.5 1.0 slice.68
  20.5 0.2 select_dynamic-update-slice_fusion.wcat
  20.7 0.0 copy-start
  20.7 1.5 copy-done
  22.2 0.0 copy-done.1
  22.2 1.3 fusion.1
  23.5 0.8 copy.25
  24.4 0.8 slice.72
  25.2 1.8 copy.24
  27.1 1.8 maximum_select_fusion
  28.9 0.1 slice.70
  29.0 0.1 slice.69
  29.0 1.7 pad_maximum_fusion.wprompt
  30.8 225.5 %shard_map.118 = bf16[4,32,160]{2,1,0:T(8,128)(2,1)} custom-call(s32[4]{0:T(128)} %order.1, s32[2]{0:T(128)} %steps.1, bf16[4,32,1280]{2,1,0:T(8,128)(2,1)} %bitcast.28, bf16[4,32,1280]{2,1,0:T(8,128)(2,1)} %bitcast.29, bf16[4,77,2048]{2,1,0:T(8,128)(2,1)} %copy.18.ptok, bf16[320,1280]{1,0:T(8,128)(2,1)} %bitcast.25, f32[9,1280]{1,0:T(8,128)} %bitcast.27, ...), custom_call_target="tpu_custom_call" | custom-call | tf_op jit(solution)/shard_map/pallas_call | solution.py:664
  256.2 1.5 copy.33
  (1 shorter events, 0.0 us)
Async XLA Ops:
  0.0 4.7 %copy-start.2 = (bf16[1,1280,3,320]{1,3,2,0:T(8,128)(2,1)S(1)}, bf16[1,1280,3,320]{1,3,2,0:T(8,128)(2,1)}, u32[]{:S(2)}) copy-start(bf16[1,1280,3,320]{1,3,2,0:T(8,128)(2,1)} %param.21) | copy-start | bytes 7372804
  17.0 5.3 %copy-start.1 = (bf16[1,2048,2,320]{1,3,2,0:T(8,128)(2,1)S(1)}, bf16[1,2048,2,320]{1,3,2,0:T(8,128)(2,1)}, u32[]{:S(2)}) copy-start(bf16[1,2048,2,320]{1,3,2,0:T(8,128)(2,1)} %param.22) | copy-start | bytes 7864324
  20.7 1.5 copy-start
